TPU v7x, 32 devices: a whole 2x2x4 slice. The times are simulated.
32 devices in a mesh: seq: 8 (over z, y), grp: 4 (over x, core).
Axes of the slice: x: 2, y: 2, z: 4, core: 2. Of those that a mesh axis runs over, the one named last changes fastest.
Arguments:
- queries: bfloat16 [8192, 1024], P(('seq', 'grp')), may hold values from -5 to 5
- key_rows: bfloat16 [8192, 128], P(('seq', 'grp')), may hold values from -5 to 5
- value_rows: bfloat16 [8192, 128], P(('seq', 'grp')), may hold values from -6 to 6
- out_grad: bfloat16 [8192, 1024], P(('seq', 'grp')), may hold values from -6 to 6
- segment: int32 [8192], P(('seq', 'grp')), may hold values from 0 to 9, never falling along the last dimension, each value on 1 to 1536 neighbouring positions
Outputs:
- attended: bfloat16 [8192, 1024], P(('seq', 'grp'))
- query_grad: bfloat16 [8192, 1024], P(('seq', 'grp'))
- key_grad: float32 [8192, 128], P(('seq', 'grp'))
- value_grad: float32 [8192, 128], P(('seq', 'grp'))
Inputs may be any that keep to these rules, and one draw needn't show every extreme that they name: `segment`: segment numbers start at 0 and never fall along the sequence; every document holds 1 to 1536 tokens, and one holds exactly 1536.
All inputs are finite; a program needn't handle non-finite values.
Results may differ from a plain program's by a relative error of at most 0.019.
Values may be sent and summed in bfloat16 or wider, within the bound.
A program may use at most 64 MiB of HBM per device.

v0:
```python
import functools
import math

import jax
import jax.numpy as jnp
from jax import lax
from jax.experimental import pallas as pl
from jax.experimental.pallas import tpu as pltpu
from jax.sharding import PartitionSpec as P

MAXDOC = 1536
AXES = ("seq", "grp")
MESH = pl.DeviceIdType.MESH
F32 = jnp.float32
BF16 = jnp.bfloat16
HIDDEN = -1e30


def dot_nt(a, b):
    return lax.dot_general(a, b, (((1,), (1,)), ((), ())), preferred_element_type=F32)


def dot_nn(a, b):
    return lax.dot_general(a, b, (((1,), (0,)), ((), ())), preferred_element_type=F32)


def kernel(
    groups, total, span,
    q_ref, k_ref, v_ref, g_ref, seg_ref,
    o_ref, dq_ref, dk_ref, dv_ref,
    keys, values, segs, qs, gs, gt, bias, scores, probs, weight,
    row_max, row_sum, row_inv, row_dot,
    gk_out, gv_out, gk_in, gv_in,
    k_send, k_recv, s_send, s_recv, v_send, v_recv, gk_send, gk_recv, gv_send, gv_recv,
):
    tokens, width = k_ref.shape
    heads = q_ref.shape[1] // width
    scale = width ** -0.5
    exponent = scale * math.log2(math.e)
    me = lax.axis_index("seq") * groups + lax.axis_index("grp")

    def device_at(distance):
        where = lax.rem(me + distance + total, total)
        return (lax.div(where, groups), lax.rem(where, groups))

    def rows(d):
        return pl.ds(pl.multiple_of(d * tokens, tokens), tokens)

    def key_copy(d):
        return pltpu.make_async_remote_copy(
            src_ref=k_ref, dst_ref=keys.at[rows(d)], send_sem=k_send.at[d], recv_sem=k_recv.at[d],
            device_id=device_at(d), device_id_type=MESH)

    def seg_copy(d):
        return pltpu.make_async_remote_copy(
            src_ref=seg_ref, dst_ref=segs.at[d], send_sem=s_send.at[d], recv_sem=s_recv.at[d],
            device_id=device_at(d), device_id_type=MESH)

    def value_copy(d):
        return pltpu.make_async_remote_copy(
            src_ref=v_ref, dst_ref=values.at[rows(d)], send_sem=v_send.at[d], recv_sem=v_recv.at[d],
            device_id=device_at(d), device_id_type=MESH)

    def key_grad_copy(d):
        return pltpu.make_async_remote_copy(
            src_ref=gk_out.at[d], dst_ref=gk_in.at[d], send_sem=gk_send.at[d],
            recv_sem=gk_recv.at[d], device_id=device_at(-d), device_id_type=MESH)

    def value_grad_copy(d):
        return pltpu.make_async_remote_copy(
            src_ref=gv_out.at[d], dst_ref=gv_in.at[d], send_sem=gv_send.at[d],
            recv_sem=gv_recv.at[d], device_id=device_at(-d), device_id_type=MESH)

    barrier = pltpu.get_barrier_semaphore()
    for d in range(1, span + 1):
        for way in (d, -d):
            pl.semaphore_signal(barrier, inc=1, device_id=device_at(way), device_id_type=MESH)

    keys[pl.ds(0, tokens), :] = k_ref[...]
    values[pl.ds(0, tokens), :] = v_ref[...]
    segs[0] = seg_ref[...]
    for h in range(heads):
        stacked = pl.ds(h * tokens, tokens)
        head = pl.ds(h * width, width)
        qs[stacked, :] = q_ref[:, head]
        gs[stacked, :] = g_ref[:, head]
        gt[:, stacked] = g_ref[:, head].T
    row_max[...] = jnp.full(row_max.shape, HIDDEN, F32)
    row_sum[...] = jnp.zeros(row_sum.shape, F32)

    pl.semaphore_wait(barrier, 2 * span)
    for d in range(1, span + 1):
        key_copy(d).start()
        seg_copy(d).start()
    for d in range(1, span + 1):
        value_copy(d).start()

    def score_pass(d, carry):
        @pl.when(d > 0)
        def _():
            key_copy(d).wait_recv()
            seg_copy(d).wait_recv()

        key_block = keys[rows(d), :]
        seg_column = jnp.broadcast_to(segs[d].astype(F32), (128, tokens)).T
        seg_key = jnp.concatenate([seg_column] * (tokens // 128), axis=1)
        key_at = lax.broadcasted_iota(jnp.int32, (tokens, tokens), 0) - d * tokens
        query_at = lax.broadcasted_iota(jnp.int32, (tokens, tokens), 1)
        first = jnp.where(me >= d, -d * tokens, tokens)
        visible = (seg_key == seg_ref[...].astype(F32)) & (key_at <= query_at) & (key_at >= first)
        bias[...] = jnp.where(visible, 0.0, HIDDEN)
        for h in range(heads):
            cols = pl.ds(h * tokens, tokens)
            score = dot_nt(key_block, qs[cols, :]) + bias[...]
            scores[rows(d), cols] = score
            top = jnp.max(score.reshape(tokens // 8, 8, tokens), axis=0)
            row_max[:, cols] = jnp.maximum(row_max[:, cols], top)
        return carry

    lax.fori_loop(0, span + 1, score_pass, 0)
    row_max[...] = jnp.broadcast_to(jnp.max(row_max[...], axis=0, keepdims=True), row_max.shape)

    def exp_pass(d, carry):
        for h in range(heads):
            cols = pl.ds(h * tokens, tokens)
            part = jnp.exp2((scores[rows(d), cols] - row_max[0:1, cols]) * exponent)
            row_sum[:, cols] += jnp.sum(part.reshape(tokens // 8, 8, tokens), axis=0)
            probs[rows(d), cols] = part.astype(BF16)
        return carry

    lax.fori_loop(0, span + 1, exp_pass, 0)
    for d in range(1, span + 1):
        value_copy(d).wait_recv()
    values_t = values[...].T
    for h in range(heads):
        cols = pl.ds(h * tokens, tokens)
        inverse = 1.0 / jnp.sum(row_sum[:, cols], axis=0, keepdims=True)
        attended = (dot_nn(values_t, probs[:, cols]) * inverse).astype(BF16)
        dot = jnp.sum(attended.astype(F32) * gt[:, cols].astype(F32), axis=0, keepdims=True)
        row_inv[:, cols] = jnp.broadcast_to(inverse, (8, tokens))
        row_dot[:, cols] = jnp.broadcast_to(dot, (8, tokens))
        o_ref[:, pl.ds(h * width, width)] = attended.T

    def grad_pass(step, carry):
        d = span - step
        value_block = values[rows(d), :]
        for h in range(heads):
            cols = pl.ds(h * tokens, tokens)
            dprob = dot_nt(value_block, gs[cols, :])
            prob = probs[rows(d), cols].astype(F32) * row_inv[0:1, cols]
            weight[:, cols] = prob.astype(BF16)
            probs[rows(d), cols] = (prob * (dprob - row_dot[0:1, cols])).astype(BF16)
        key_part = dot_nn(probs[rows(d), :], qs[...]) * scale
        value_part = dot_nn(weight[...], gs[...])

        @pl.when(d > 0)
        def _():
            gk_out[d] = key_part.astype(BF16)
            gv_out[d] = value_part.astype(BF16)
            key_grad_copy(d).start()
            value_grad_copy(d).start()

        @pl.when(d == 0)
        def _():
            dk_ref[...] = key_part
            dv_ref[...] = value_part

        return carry

    lax.fori_loop(0, span + 1, grad_pass, 0)
    keys_t = keys[...].T
    for h in range(heads):
        cols = pl.ds(h * tokens, tokens)
        grad = (dot_nn(keys_t, probs[:, cols]) * scale).astype(BF16)
        dq_ref[:, pl.ds(h * width, width)] = grad.T
    for d in range(span, 0, -1):
        key_grad_copy(d).wait_recv()
        value_grad_copy(d).wait_recv()
        dk_ref[...] += gk_in[d].astype(F32)
        dv_ref[...] += gv_in[d].astype(F32)
    for d in range(1, span + 1):
        key_copy(d).wait_send()
        seg_copy(d).wait_send()
        value_copy(d).wait_send()
        key_grad_copy(d).wait_send()
        value_grad_copy(d).wait_send()


def on_device(queries, key_rows, value_rows, out_grad, segment):
    tokens, width = key_rows.shape
    heads = queries.shape[1] // width
    groups = lax.axis_size("grp")
    total = groups * lax.axis_size("seq")
    span = -(-MAXDOC // tokens)
    blocks = span + 1
    stacked = heads * tokens
    seg_rows = segment.reshape(1, tokens)
    vmem = pl.BlockSpec(memory_space=pltpu.VMEM)
    sems = pltpu.SemaphoreType.DMA((blocks,))
    return pl.pallas_call(
        functools.partial(kernel, groups, total, span),
        out_shape=(
            jax.ShapeDtypeStruct(queries.shape, BF16),
            jax.ShapeDtypeStruct(queries.shape, BF16),
            jax.ShapeDtypeStruct(key_rows.shape, F32),
            jax.ShapeDtypeStruct(key_rows.shape, F32),
        ),
        in_specs=[vmem] * 5,
        out_specs=(vmem,) * 4,
        scratch_shapes=[
            pltpu.VMEM((blocks * tokens, width), BF16),
            pltpu.VMEM((blocks * tokens, width), BF16),
            pltpu.VMEM((blocks, 1, tokens), jnp.int32),
            pltpu.VMEM((stacked, width), BF16),
            pltpu.VMEM((stacked, width), BF16),
            pltpu.VMEM((width, stacked), BF16),
            pltpu.VMEM((tokens, tokens), F32),
            pltpu.VMEM((blocks * tokens, stacked), F32),
            pltpu.VMEM((blocks * tokens, stacked), BF16),
            pltpu.VMEM((tokens, stacked), BF16),
            pltpu.VMEM((8, stacked), F32),
            pltpu.VMEM((8, stacked), F32),
            pltpu.VMEM((8, stacked), F32),
            pltpu.VMEM((8, stacked), F32),
            pltpu.VMEM((blocks, tokens, width), BF16),
            pltpu.VMEM((blocks, tokens, width), BF16),
            pltpu.VMEM((blocks, tokens, width), BF16),
            pltpu.VMEM((blocks, tokens, width), BF16),
        ]
        + [sems] * 10,
        compiler_params=pltpu.CompilerParams(
            collective_id=0, has_side_effects=True, vmem_limit_bytes=60 * 1024 * 1024
        ),
    )(queries, key_rows, value_rows, out_grad, seg_rows)


def solution(mesh):
    in_specs = (P(AXES, None), P(AXES, None), P(AXES, None), P(AXES, None), P(AXES))
    out_specs = (P(AXES, None),) * 4
    return jax.shard_map(
        on_device, mesh=mesh, in_specs=in_specs, out_specs=out_specs, check_vma=False
    )
```

profile of v0, /device:TPU:7, one launch (start us, length us, event | category | flops | bytes accessed | tf_op | source)
XLA Modules:
  0.0 49.2 jit_solution(7084024917412344723)
XLA Ops:
  0.6 44.0 %shard_map.84 = (bf16[256,1024]{1,0:T(8,128)(2,1)}, bf16[256,1024]{1,0:T(8,128)(2,1)}, f32[256,128]{1,0:T(8,128)}, f32[256,128]{1,0:T(8,128)}) custom-call(bf16[256,1024]{1,0:T(8,128)(2,1)} %q_ref.1, bf16[256,128]{1,0:T(8,128)(2,1)} %k_ref.1, bf16[256,128]{1,0:T(8,128)(2,1)} %v_ref.1, bf16[256,1024]{1,0:T(8,128)(2,1)} %g_ref.1, s32[1,256]{1,0:T(1,128)} %bitcast.1), custom_call_target="tpu_custom_call" | custom-call | tf_op jit(solution)/shard_map/pallas_call | solution.py:200
  44.6 0.0 copy-start
  44.7 1.9 %copy.13 = bf16[256,1024]{1,0:T(8,128)(2,1)} copy(bf16[256,1024]{1,0:T(8,128)(2,1)} %get-tuple-element.8) | data formatting | bytes 1048576
  46.6 0.0 copy-done
  46.6 0.0 copy-start.2
  46.6 0.8 %copy.14 = bf16[256,1024]{1,0:T(8,128)(2,1)} copy(bf16[256,1024]{1,0:T(8,128)(2,1)S(1)} %copy-done) | data formatting | bytes 1048576
  47.4 0.2 copy-done.2
  47.6 0.0 copy-start.1
  47.6 0.7 %copy.15 = f32[256,128]{1,0:T(8,128)} copy(f32[256,128]{1,0:T(8,128)S(1)} %copy-done.2) | data formatting | bytes 262144
  48.3 0.3 copy-done.1
  48.6 0.7 %copy.16 = f32[256,128]{1,0:T(8,128)} copy(f32[256,128]{1,0:T(8,128)S(1)} %copy-done.1) | data formatting | bytes 262144
Async XLA Ops:
  44.6 1.9 %copy-start = (bf16[256,1024]{1,0:T(8,128)(2,1)S(1)}, bf16[256,1024]{1,0:T(8,128)(2,1)}, u32[]{:S(2)}) copy-start(bf16[256,1024]{1,0:T(8,128)(2,1)} %get-tuple-element.9) | copy-start | bytes 1572868
  46.6 1.0 %copy-start.2 = (f32[256,128]{1,0:T(8,128)S(1)}, f32[256,128]{1,0:T(8,128)}, u32[]{:S(2)}) copy-start(f32[256,128]{1,0:T(8,128)} %get-tuple-element.10) | copy-start | bytes 393220
  47.6 1.0 %copy-start.1 = (f32[256,128]{1,0:T(8,128)S(1)}, f32[256,128]{1,0:T(8,128)}, u32[]{:S(2)}) copy-start(f32[256,128]{1,0:T(8,128)} %get-tuple-element.11) | copy-start | bytes 393220
where the time goes:
time: 49.4 us; the launch traced here: 49.2 us
  Pallas kernels  44 us (89%)
  local copies, waits for them, and re-layouts  4.56 us (9%)
  between operations  0.65 us (1%)
    pallas_call x1, Pallas kernels, on_device(): pl.pallas_call(functools.partial(kernel, groups, total, span), out_shape=...  44 us
    unnamed x10, local copies, waits for them, and re-layouts  4.56 us

commit v1 on v0

v1 whole, which is shorter than its diff:
```python
import functools
import math

import jax
import jax.numpy as jnp
from jax import lax
from jax.experimental import pallas as pl
from jax.experimental.pallas import tpu as pltpu
from jax.sharding import PartitionSpec as P

MAXDOC = 1536
AXES = ("seq", "grp")
MESH = pl.DeviceIdType.MESH
F32 = jnp.float32
BF16 = jnp.bfloat16
HIDDEN = -1e30


def dot_nt(a, b):
    return lax.dot_general(a, b, (((1,), (1,)), ((), ())), preferred_element_type=F32)


def dot_nn(a, b):
    return lax.dot_general(a, b, (((1,), (0,)), ((), ())), preferred_element_type=F32)


def kernel(
    groups, total, span,
    q_hbm, k_hbm, v_hbm, g_hbm, seg_hbm,
    o_hbm, dq_hbm, dk_hbm, dv_hbm,
    keys, values, segs, qs, gs, gt, bias, probs, o_buf, dq_buf, dk_buf, dv_buf,
    row_max, tops, sums, row_dot,
    gk_odd, gv_odd, gk_pair, gv_pair, gk_out, gv_out, gk_in, gv_in,
    local, o_sem, dq_sem, d_sem,
    k_send, k_recv, s_send, s_recv, v_send, v_recv, kf_send, vf_send,
    gkp_send, gkp_recv, gvp_send, gvp_recv, gk_send, gk_recv, gv_send, gv_recv,
):
    tokens, width = k_hbm.shape
    heads = q_hbm.shape[1] // width
    half = span // 2
    scale = width ** -0.5
    exponent = scale * math.log2(math.e)
    me = lax.axis_index("seq") * groups + lax.axis_index("grp")
    parity = lax.rem(me, 2)
    partner = me + 1 - 2 * parity

    def at(where):
        return (lax.div(where, groups), lax.rem(where, groups))

    def rows(d):
        return pl.ds(pl.multiple_of(d * tokens, tokens), tokens)

    def remote(src, dst, send, recv, where):
        return pltpu.make_async_remote_copy(
            src_ref=src, dst_ref=dst, send_sem=send, recv_sem=recv,
            device_id=at(where), device_id_type=MESH)

    def key_copy(d):
        return remote(keys.at[rows(0)], keys.at[rows(d)], k_send.at[d], k_recv.at[d], me + d)

    def value_copy(d):
        return remote(values.at[rows(0)], values.at[rows(d)], v_send.at[d], v_recv.at[d], me + d)

    def seg_copy(d):
        return remote(segs.at[0], segs.at[d], s_send.at[d], s_recv.at[d], me + d)

    def key_pass_on(j):
        return remote(keys.at[rows(2 * j + 2 * parity)], keys.at[rows(2 * j + 1)],
                      kf_send.at[j], k_recv.at[2 * j + 1], partner)

    def value_pass_on(j):
        return remote(values.at[rows(2 * j + 2 * parity)], values.at[rows(2 * j + 1)],
                      vf_send.at[j], v_recv.at[2 * j + 1], partner)

    def pair_copy(odd, pair, send, recv, j):
        return remote(odd.at[j], pair.at[j], send.at[j], recv.at[j], partner)

    def total_copy(out, into, send, recv, j):
        return remote(out.at[j], into.at[j], send.at[j], recv.at[j], me - 2 * (j + 1))

    barrier = pltpu.get_barrier_semaphore()
    expected = 0
    for d in range(1, span + 1):
        for way in (d, -d):
            inside = (me + way >= 0) & (me + way < total)
            expected = expected + inside.astype(jnp.int32)

            @pl.when(inside)
            def _():
                pl.semaphore_signal(barrier, inc=1, device_id=at(me + way), device_id_type=MESH)

    key_load = pltpu.make_async_copy(k_hbm, keys.at[pl.ds(0, tokens)], local.at[0])
    seg_load = pltpu.make_async_copy(seg_hbm, segs.at[0], local.at[1])
    value_load = pltpu.make_async_copy(v_hbm, values.at[pl.ds(0, tokens)], local.at[2])
    key_load.start()
    seg_load.start()
    value_load.start()
    loads_q = []
    loads_g = []
    for h in range(heads):
        stacked = pl.ds(h * tokens, tokens)
        head = pl.ds(h * width, width)
        loads_q.append(pltpu.make_async_copy(q_hbm.at[:, head], qs.at[stacked], local.at[3 + h]))
        loads_g.append(pltpu.make_async_copy(g_hbm.at[:, head], gs.at[stacked], local.at[3 + heads + h]))
    for load in loads_q + loads_g:
        load.start()

    for d in range(1, span + 1):
        @pl.when(me < d)
        def _():
            keys[pl.ds(d * tokens, tokens), :] = jnp.zeros((tokens, width), BF16)
            values[pl.ds(d * tokens, tokens), :] = jnp.zeros((tokens, width), BF16)
            segs[d] = jnp.zeros((1, tokens), jnp.int32)

    key_load.wait()
    seg_load.wait()
    value_load.wait()
    pl.semaphore_wait(barrier, expected)

    @pl.when(parity == 0)
    def _():
        key_pass_on(0).start()

    for d in range(2, span + 1, 2):
        @pl.when(me + d < total)
        def _():
            key_copy(d).start()

    for d in range(1, span + 1):
        @pl.when(me + d < total)
        def _():
            seg_copy(d).start()

    @pl.when(parity == 0)
    def _():
        value_pass_on(0).start()

    for d in range(2, span + 1, 2):
        @pl.when(me + d < total)
        def _():
            value_copy(d).start()

    row_max[...] = jnp.full(row_max.shape, HIDDEN, F32)
    for load in loads_q + loads_g:
        load.wait()
    for h in range(heads):
        stacked = pl.ds(h * tokens, tokens)
        gt[:, stacked] = gs[stacked, :].T

    def score_pass(s, carry):
        odd = lax.rem(s, 2)
        d = jnp.where(s == 0, 0, s + 2 * odd - 1)
        j = lax.div(d, 2) - parity

        @pl.when((d > 0) & (me >= d))
        def _():
            key_copy(d).wait_recv()
            seg_copy(d).wait_recv()

        @pl.when((odd == 1) & (me >= d) & (j < half))
        def _():
            key_pass_on(j).start()

        key_block = keys[rows(d), :]
        seg_column = jnp.broadcast_to(segs[d].astype(F32), (128, tokens)).T
        seg_key = jnp.concatenate([seg_column] * (tokens // 128), axis=1)
        key_at = lax.broadcasted_iota(jnp.int32, (tokens, tokens), 0) - d * tokens
        query_at = lax.broadcasted_iota(jnp.int32, (tokens, tokens), 1)
        first = jnp.where(me >= d, -d * tokens, tokens)
        visible = (seg_key == segs[0].astype(F32)) & (key_at <= query_at) & (key_at >= first)
        bias[...] = jnp.where(visible, 0.0, HIDDEN)
        for h in range(heads):
            cols = pl.ds(h * tokens, tokens)
            score = dot_nt(key_block, qs[cols, :]) + bias[...]
            top = jnp.max(score, axis=0, keepdims=True)
            top = jnp.maximum(row_max[0:1, cols], top)
            part = jnp.exp2((score - top) * exponent)
            row_max[:, cols] = jnp.broadcast_to(top, (8, tokens))
            tops[d, :, cols] = jnp.broadcast_to(top, (8, tokens))
            sums[d, :, cols] = jnp.sum(part.reshape(tokens // 8, 8, tokens), axis=0)
            probs[rows(d), cols] = part.astype(BF16)
        return carry

    lax.fori_loop(0, span + 1, score_pass, 0)
    for h in range(heads):
        cols = pl.ds(h * tokens, tokens)
        whole = jnp.zeros((8, tokens), F32)
        for d in range(span + 1):
            part = jnp.exp2((tops[d, :, cols] - row_max[:, cols]) * exponent)
            tops[d, :, cols] = part
            whole += part * sums[d, :, cols]
        inverse = jnp.broadcast_to(1.0 / jnp.sum(whole, axis=0, keepdims=True), (8, tokens))
        for d in range(span + 1):
            tops[d, :, cols] *= inverse

    order = [d for m in range(half, 0, -1) for d in (2 * m - 1, 2 * m)]
    order = [5, 3, 6, 1, 4, 2, 0] if span == 6 else order + [0]

    def block_at(s):
        d = order[-1]
        for i in range(len(order) - 1):
            d = jnp.where(s == i, order[i], d)
        return d

    def hand_out(d, part, odd_ref, pair_ref, out_ref, sum_ref, p_send, p_recv, t_send, into, t_recv):
        sum_ref[...] = part
        j = lax.div(d, 2)
        is_odd = lax.rem(d, 2) == 1

        @pl.when(is_odd & (me >= d))
        def _():
            odd_ref[j] = sum_ref[...].astype(BF16)
            pair_copy(odd_ref, pair_ref, p_send, p_recv, j).start()

        i = j - parity

        @pl.when(jnp.logical_not(is_odd) & (me >= d) & (i >= 0) & (i < half))
        def _():
            pair_copy(odd_ref, pair_ref, p_send, p_recv, i).wait_recv()
            sum_ref[...] += pair_ref[i].astype(F32)

        @pl.when(jnp.logical_not(is_odd) & (d > 0) & (me >= d))
        def _():
            out_ref[j - 1] = sum_ref[...].astype(BF16)
            total_copy(out_ref, into, t_send, t_recv, j - 1).start()

    def value_grad_pass(s, carry):
        d = block_at(s)
        e = 2 * s + 2

        @pl.when((s < half) & (me >= e))
        def _():
            value_copy(e).wait_recv()

        @pl.when((s < half) & (me >= e) & (s + 1 - parity < half))
        def _():
            value_pass_on(s + 1 - parity).start()

        for h in range(heads):
            cols = pl.ds(h * tokens, tokens)
            prob = probs[rows(d), cols].astype(F32) * tops[d, 0:1, cols]
            probs[rows(d), cols] = prob.astype(BF16)
        part = dot_nn(probs[rows(d), :], gs[...])
        hand_out(d, part, gv_odd, gv_pair, gv_out, dv_buf, gvp_send, gvp_recv, gv_send, gv_in, gv_recv)
        return carry

    lax.fori_loop(0, span + 1, value_grad_pass, 0)
    for d in range(1, span + 1, 2):
        @pl.when(me >= d)
        def _():
            value_copy(d).wait_recv()

    values_t = values[...].T
    o_copies = []
    for h in range(heads):
        cols = pl.ds(h * tokens, tokens)
        head = pl.ds(h * width, width)
        attended = dot_nn(values_t, probs[:, cols]).astype(BF16)
        dot = jnp.sum(attended.astype(F32) * gt[:, cols].astype(F32), axis=0, keepdims=True)
        row_dot[:, cols] = jnp.broadcast_to(dot, (8, tokens))
        o_buf[:, head] = attended.T
    o_copy = pltpu.make_async_copy(o_buf, o_hbm, o_sem)
    o_copy.start()

    def key_grad_pass(s, carry):
        d = block_at(s)
        value_block = values[rows(d), :]
        for h in range(heads):
            cols = pl.ds(h * tokens, tokens)
            dprob = dot_nt(value_block, gs[cols, :])
            prob = probs[rows(d), cols].astype(F32)
            probs[rows(d), cols] = (prob * (dprob - row_dot[0:1, cols])).astype(BF16)
        part = dot_nn(probs[rows(d), :], qs[...]) * scale
        hand_out(d, part, gk_odd, gk_pair, gk_out, dk_buf, gkp_send, gkp_recv, gk_send, gk_in, gk_recv)
        return carry

    lax.fori_loop(0, span + 1, key_grad_pass, 0)
    keys_t = keys[...].T
    for h in range(heads):
        cols = pl.ds(h * tokens, tokens)
        grad = (dot_nn(keys_t, probs[:, cols]) * scale).astype(BF16)
        dq_buf[:, pl.ds(h * width, width)] = grad.T
    dq_copy = pltpu.make_async_copy(dq_buf, dq_hbm, dq_sem)
    dq_copy.start()

    for j in range(half - 1, -1, -1):
        @pl.when(me + 2 * (j + 1) < total)
        def _():
            total_copy(gv_out, gv_in, gv_send, gv_recv, j).wait_recv()
            dv_buf[...] += gv_in[j].astype(F32)

    dv_copy = pltpu.make_async_copy(dv_buf, dv_hbm, d_sem.at[0])
    dv_copy.start()
    for j in range(half - 1, -1, -1):
        @pl.when(me + 2 * (j + 1) < total)
        def _():
            total_copy(gk_out, gk_in, gk_send, gk_recv, j).wait_recv()
            dk_buf[...] += gk_in[j].astype(F32)

    dk_copy = pltpu.make_async_copy(dk_buf, dk_hbm, d_sem.at[1])
    dk_copy.start()

    for d in range(1, span + 1):
        @pl.when(me + d < total)
        def _():
            seg_copy(d).wait_send()
            if d % 2 == 0:
                key_copy(d).wait_send()
                value_copy(d).wait_send()
    for j in range(half):
        @pl.when(me >= 2 * j + 2 * parity)
        def _():
            key_pass_on(j).wait_send()
            value_pass_on(j).wait_send()

        @pl.when(me >= 2 * j + 1)
        def _():
            pair_copy(gv_odd, gv_pair, gvp_send, gvp_recv, j).wait_send()
            pair_copy(gk_odd, gk_pair, gkp_send, gkp_recv, j).wait_send()

        @pl.when(me >= 2 * j + 2)
        def _():
            total_copy(gv_out, gv_in, gv_send, gv_recv, j).wait_send()
            total_copy(gk_out, gk_in, gk_send, gk_recv, j).wait_send()
    o_copy.wait()
    dq_copy.wait()
    dv_copy.wait()
    dk_copy.wait()


def on_device(queries, key_rows, value_rows, out_grad, segment):
    tokens, width = key_rows.shape
    heads = queries.shape[1] // width
    groups = lax.axis_size("grp")
    total = groups * lax.axis_size("seq")
    span = -(-MAXDOC // tokens)
    span += span % 2
    blocks = span + 1
    half = span // 2
    stacked = heads * tokens
    seg_rows = segment.reshape(1, tokens)
    anywhere = pl.BlockSpec(memory_space=pl.ANY)
    sem = pltpu.SemaphoreType.DMA
    block = pltpu.VMEM((half, tokens, width), BF16)
    return pl.pallas_call(
        functools.partial(kernel, groups, total, span),
        out_shape=(
            jax.ShapeDtypeStruct(queries.shape, BF16),
            jax.ShapeDtypeStruct(queries.shape, BF16),
            jax.ShapeDtypeStruct(key_rows.shape, F32),
            jax.ShapeDtypeStruct(key_rows.shape, F32),
        ),
        in_specs=[anywhere] * 5,
        out_specs=(anywhere,) * 4,
        scratch_shapes=[
            pltpu.VMEM((blocks * tokens, width), BF16),
            pltpu.VMEM((blocks * tokens, width), BF16),
            pltpu.VMEM((blocks, 1, tokens), jnp.int32),
            pltpu.VMEM((stacked, width), BF16),
            pltpu.VMEM((stacked, width), BF16),
            pltpu.VMEM((width, stacked), BF16),
            pltpu.VMEM((tokens, tokens), F32),
            pltpu.VMEM((blocks * tokens, stacked), BF16),
            pltpu.VMEM(queries.shape, BF16),
            pltpu.VMEM(queries.shape, BF16),
            pltpu.VMEM(key_rows.shape, F32),
            pltpu.VMEM(key_rows.shape, F32),
            pltpu.VMEM((8, stacked), F32),
            pltpu.VMEM((blocks, 8, stacked), F32),
            pltpu.VMEM((blocks, 8, stacked), F32),
            pltpu.VMEM((8, stacked), F32),
        ]
        + [block] * 8
        + [sem((3 + 2 * heads,)), sem, sem, sem((2,))]
        + [sem((blocks,))] * 6
        + [sem((half,))] * 10,
        compiler_params=pltpu.CompilerParams(
            collective_id=0, has_side_effects=True, vmem_limit_bytes=60 * 1024 * 1024
        ),
    )(queries, key_rows, value_rows, out_grad, seg_rows)


def solution(mesh):
    in_specs = (P(AXES, None), P(AXES, None), P(AXES, None), P(AXES, None), P(AXES))
    out_specs = (P(AXES, None),) * 4
    return jax.shard_map(
        on_device, mesh=mesh, in_specs=in_specs, out_specs=out_specs, check_vma=False
    )
```

time: 49.4 us -> 35.7 us (0.72)
  Pallas kernels: 44 us -> 30.1 us
    pallas_call x1, Pallas kernels: 44 us -> 30.1 us  [on_device(): pl.pallas_call(functools.partial(kernel, groups, total, span), out_shape=...]
where the time goes in v1:
time: 35.7 us; the launch traced here: 35.4 us
  Pallas kernels  30.1 us (84%)
  local copies, waits for them, and re-layouts  4.56 us (13%)
  between operations  0.65 us (2%)
    pallas_call x1, Pallas kernels, on_device(): pl.pallas_call(functools.partial(kernel, groups, total, span), out_shape=...  30.1 us
    unnamed x10, local copies, waits for them, and re-layouts  4.56 us

profile of v1, /device:TPU:7, one launch (start us, length us, event | category | flops | bytes accessed | tf_op | source)
XLA Modules:
  0.0 35.4 jit_solution(18175245791563131637)
XLA Ops:
  0.6 30.1 %shard_map.84 = (bf16[256,1024]{1,0:T(8,128)(2,1)}, bf16[256,1024]{1,0:T(8,128)(2,1)}, f32[256,128]{1,0:T(8,128)}, f32[256,128]{1,0:T(8,128)}) custom-call(bf16[256,1024]{1,0:T(8,128)(2,1)} %q_hbm.1, bf16[256,128]{1,0:T(8,128)(2,1)} %k_hbm.1, bf16[256,128]{1,0:T(8,128)(2,1)} %v_hbm.1, bf16[256,1024]{1,0:T(8,128)(2,1)} %g_hbm.1, s32[1,256]{1,0:T(1,128)} %bitcast.1), custom_call_target="tpu_custom_call" | custom-call | tf_op jit(solution)/shard_map/pallas_call | solution.py:345
  30.8 0.0 copy-start
  30.8 1.9 %copy.13 = bf16[256,1024]{1,0:T(8,128)(2,1)} copy(bf16[256,1024]{1,0:T(8,128)(2,1)} %get-tuple-element.8) | data formatting | bytes 1048576
  32.7 0.0 copy-done
  32.7 0.0 copy-start.2
  32.7 0.8 %copy.14 = bf16[256,1024]{1,0:T(8,128)(2,1)} copy(bf16[256,1024]{1,0:T(8,128)(2,1)S(1)} %copy-done) | data formatting | bytes 1048576
  33.5 0.2 copy-done.2
  33.7 0.0 copy-start.1
  33.7 0.7 %copy.15 = f32[256,128]{1,0:T(8,128)} copy(f32[256,128]{1,0:T(8,128)S(1)} %copy-done.2) | data formatting | bytes 262144
  34.4 0.3 copy-done.1
  34.7 0.7 %copy.16 = f32[256,128]{1,0:T(8,128)} copy(f32[256,128]{1,0:T(8,128)S(1)} %copy-done.1) | data formatting | bytes 262144
Async XLA Ops:
  30.8 1.9 %copy-start = (bf16[256,1024]{1,0:T(8,128)(2,1)S(1)}, bf16[256,1024]{1,0:T(8,128)(2,1)}, u32[]{:S(2)}) copy-start(bf16[256,1024]{1,0:T(8,128)(2,1)} %get-tuple-element.9) | copy-start | bytes 1572868
  32.7 1.0 %copy-start.2 = (f32[256,128]{1,0:T(8,128)S(1)}, f32[256,128]{1,0:T(8,128)}, u32[]{:S(2)}) copy-start(f32[256,128]{1,0:T(8,128)} %get-tuple-element.10) | copy-start | bytes 393220
  33.7 1.0 %copy-start.1 = (f32[256,128]{1,0:T(8,128)S(1)}, f32[256,128]{1,0:T(8,128)}, u32[]{:S(2)}) copy-start(f32[256,128]{1,0:T(8,128)} %get-tuple-element.11) | copy-start | bytes 393220

commit v2 on v1

--- a/solution.py
+++ b/solution.py
@@ -27,11 +27,11 @@
 def kernel(
     groups, total, span,
     q_hbm, k_hbm, v_hbm, g_hbm, seg_hbm,
-    o_hbm, dq_hbm, dk_hbm, dv_hbm,
-    keys, values, segs, qs, gs, gt, bias, probs, o_buf, dq_buf, dk_buf, dv_buf,
+    o_buf, dq_buf, dk_buf, dv_buf,
+    keys, values, segs, qs, gs, gt, bias, probs,
     row_max, tops, sums, row_dot,
     gk_odd, gv_odd, gk_pair, gv_pair, gk_out, gv_out, gk_in, gv_in,
-    local, o_sem, dq_sem, d_sem,
+    local,
     k_send, k_recv, s_send, s_recv, v_send, v_recv, kf_send, vf_send,
     gkp_send, gkp_recv, gvp_send, gvp_recv, gk_send, gk_recv, gv_send, gv_recv,
 ):
@@ -251,7 +251,6 @@
             value_copy(d).wait_recv()
 
     values_t = values[...].T
-    o_copies = []
     for h in range(heads):
         cols = pl.ds(h * tokens, tokens)
         head = pl.ds(h * width, width)
@@ -259,8 +258,6 @@
         dot = jnp.sum(attended.astype(F32) * gt[:, cols].astype(F32), axis=0, keepdims=True)
         row_dot[:, cols] = jnp.broadcast_to(dot, (8, tokens))
         o_buf[:, head] = attended.T
-    o_copy = pltpu.make_async_copy(o_buf, o_hbm, o_sem)
-    o_copy.start()
 
     def key_grad_pass(s, carry):
         d = block_at(s)
@@ -280,8 +277,6 @@
         cols = pl.ds(h * tokens, tokens)
         grad = (dot_nn(keys_t, probs[:, cols]) * scale).astype(BF16)
         dq_buf[:, pl.ds(h * width, width)] = grad.T
-    dq_copy = pltpu.make_async_copy(dq_buf, dq_hbm, dq_sem)
-    dq_copy.start()
 
     for j in range(half - 1, -1, -1):
         @pl.when(me + 2 * (j + 1) < total)
@@ -289,16 +284,12 @@
             total_copy(gv_out, gv_in, gv_send, gv_recv, j).wait_recv()
             dv_buf[...] += gv_in[j].astype(F32)
 
-    dv_copy = pltpu.make_async_copy(dv_buf, dv_hbm, d_sem.at[0])
-    dv_copy.start()
     for j in range(half - 1, -1, -1):
         @pl.when(me + 2 * (j + 1) < total)
         def _():
             total_copy(gk_out, gk_in, gk_send, gk_recv, j).wait_recv()
             dk_buf[...] += gk_in[j].astype(F32)
 
-    dk_copy = pltpu.make_async_copy(dk_buf, dk_hbm, d_sem.at[1])
-    dk_copy.start()
 
     for d in range(1, span + 1):
         @pl.when(me + d < total)
@@ -322,10 +313,6 @@
         def _():
             total_copy(gv_out, gv_in, gv_send, gv_recv, j).wait_send()
             total_copy(gk_out, gk_in, gk_send, gk_recv, j).wait_send()
-    o_copy.wait()
-    dq_copy.wait()
-    dv_copy.wait()
-    dk_copy.wait()
 
 
 def on_device(queries, key_rows, value_rows, out_grad, segment):
@@ -342,16 +329,16 @@
     anywhere = pl.BlockSpec(memory_space=pl.ANY)
     sem = pltpu.SemaphoreType.DMA
     block = pltpu.VMEM((half, tokens, width), BF16)
-    return pl.pallas_call(
+    results = pl.pallas_call(
         functools.partial(kernel, groups, total, span),
         out_shape=(
-            jax.ShapeDtypeStruct(queries.shape, BF16),
-            jax.ShapeDtypeStruct(queries.shape, BF16),
-            jax.ShapeDtypeStruct(key_rows.shape, F32),
-            jax.ShapeDtypeStruct(key_rows.shape, F32),
+            pltpu.VMEM(queries.shape, BF16),
+            pltpu.VMEM(queries.shape, BF16),
+            pltpu.VMEM(key_rows.shape, F32),
+            pltpu.VMEM(key_rows.shape, F32),
         ),
         in_specs=[anywhere] * 5,
-        out_specs=(anywhere,) * 4,
+        out_specs=(pl.BlockSpec(memory_space=pltpu.VMEM),) * 4,
         scratch_shapes=[
             pltpu.VMEM((blocks * tokens, width), BF16),
             pltpu.VMEM((blocks * tokens, width), BF16),
@@ -361,23 +348,45 @@
             pltpu.VMEM((width, stacked), BF16),
             pltpu.VMEM((tokens, tokens), F32),
             pltpu.VMEM((blocks * tokens, stacked), BF16),
-            pltpu.VMEM(queries.shape, BF16),
-            pltpu.VMEM(queries.shape, BF16),
-            pltpu.VMEM(key_rows.shape, F32),
-            pltpu.VMEM(key_rows.shape, F32),
             pltpu.VMEM((8, stacked), F32),
             pltpu.VMEM((blocks, 8, stacked), F32),
             pltpu.VMEM((blocks, 8, stacked), F32),
             pltpu.VMEM((8, stacked), F32),
         ]
         + [block] * 8
-        + [sem((3 + 2 * heads,)), sem, sem, sem((2,))]
+        + [sem((3 + 2 * heads,))]
         + [sem((blocks,))] * 6
         + [sem((half,))] * 10,
         compiler_params=pltpu.CompilerParams(
-            collective_id=0, has_side_effects=True, vmem_limit_bytes=60 * 1024 * 1024
+            collective_id=0, has_side_effects=True, vmem_limit_bytes=40 * 1024 * 1024
         ),
-    )(queries, key_rows, value_rows, out_grad, seg_rows)
+    )(*[
+        pltpu.with_memory_space_constraint(a, pltpu.HBM)
+        for a in (queries, key_rows, value_rows, out_grad, seg_rows)
+    ])
+    return write_back(results)
+
+
+def store(*refs):
+    count = (len(refs) - 1) // 2
+    copies = [pltpu.make_async_copy(refs[i], refs[count + i], refs[-1].at[i]) for i in range(count)]
+    for copy in copies:
+        copy.start()
+    for copy in copies:
+        copy.wait()
+
+
+def write_back(results):
+    anywhere = pl.BlockSpec(memory_space=pl.ANY)
+    held = [pltpu.with_memory_space_constraint(r, pltpu.VMEM) for r in results]
+    return pl.pallas_call(
+        store,
+        out_shape=tuple(jax.ShapeDtypeStruct(r.shape, r.dtype) for r in results),
+        in_specs=[pl.BlockSpec(memory_space=pltpu.VMEM)] * len(results),
+        out_specs=(anywhere,) * len(results),
+        scratch_shapes=[pltpu.SemaphoreType.DMA((len(results),))],
+        compiler_params=pltpu.CompilerParams(vmem_limit_bytes=4 * 1024 * 1024),
+    )(*held)
 
 
 def solution(mesh):

time: 35.7 us -> 31.6 us (0.89)
  local copies, waits for them, and re-layouts: 4.56 us -> 0 us
  Pallas kernels: 30.1 us -> 30.6 us
    unnamed x10 -> x0, local copies, waits for them, and re-layouts: 4.56 us -> none
    pallas_call x0 -> x1, Pallas kernels: none -> 1.08 us  [write_back(): pl.pallas_call(store, out_shape=tuple((jax.ShapeDtypeStruct(r.shape, r.dt...]
    pallas_call x1, Pallas kernels: 30.1 us -> 29.5 us  [on_device(): pl.pallas_call(functools.partial(kernel, groups, total, span), out_shape=...]
where the time goes in v2:
time: 31.6 us; the launch traced here: 31.3 us
  Pallas kernels  30.6 us (97%)
  between operations  0.64 us (2%)
    pallas_call x1, Pallas kernels, on_device(): pl.pallas_call(functools.partial(kernel, groups, total, span), out_shape=...  29.5 us
    pallas_call x1, Pallas kernels, write_back(): pl.pallas_call(store, out_shape=tuple((jax.ShapeDtypeStruct(r.shape, r.dt...  1.08 us

profile of v2, /device:TPU:7, one launch (start us, length us, event | category | flops | bytes accessed | tf_op | source)
XLA Modules:
  0.0 31.3 jit_solution(13030431074838912401)
XLA Ops:
  0.6 29.5 %shard_map.84 = (bf16[256,1024]{1,0:T(8,128)(2,1)S(1)}, bf16[256,1024]{1,0:T(8,128)(2,1)S(1)}, f32[256,128]{1,0:T(8,128)S(1)}, f32[256,128]{1,0:T(8,128)S(1)}) custom-call(bf16[256,1024]{1,0:T(8,128)(2,1)} %q_hbm.1, bf16[256,128]{1,0:T(8,128)(2,1)} %k_hbm.1, bf16[256,128]{1,0:T(8,128)(2,1)} %v_hbm.1, bf16[256,1024]{1,0:T(8,128)(2,1)} %g_hbm.1, s32[1,256]{1,0:T(1,128)} %bitcast.1), custom_call_target="tpu_custom_call" | custom-call | tf_op jit(solution)/shard_map/pallas_call | solution.py:332
  30.2 1.1 %shard_map.85 = (bf16[256,1024]{1,0:T(8,128)(2,1)}, bf16[256,1024]{1,0:T(8,128)(2,1)}, f32[256,128]{1,0:T(8,128)}, f32[256,128]{1,0:T(8,128)}) custom-call(bf16[256,1024]{1,0:T(8,128)(2,1)S(1)} %get-tuple-element.8.refs_0_, bf16[256,1024]{1,0:T(8,128)(2,1)S(1)} %get-tuple-element.9.refs_1_, f32[256,128]{1,0:T(8,128)S(1)} %get-tuple-element.10.refs_2_, ...), custom_call_target="tpu_custom_call" | custom-call | tf_op jit(solution)/shard_map/pallas_call | solution.py:382

commit v3 on v2

--- a/solution.py
+++ b/solution.py
@@ -14,6 +14,7 @@
 F32 = jnp.float32
 BF16 = jnp.bfloat16
 HIDDEN = -1e30
+SAME = 8192.0
 
 
 def dot_nt(a, b):
@@ -28,8 +29,8 @@
     groups, total, span,
     q_hbm, k_hbm, v_hbm, g_hbm, seg_hbm,
     o_buf, dq_buf, dk_buf, dv_buf,
-    keys, values, segs, qs, gs, gt, bias, probs,
-    row_max, tops, sums, row_dot,
+    keys, values, segs, qs, gs, qt, gt, hots, marks_t, scores, probs, dscores, value_parts,
+    row_max, row_inv, row_dot,
     gk_odd, gv_odd, gk_pair, gv_pair, gk_out, gv_out, gk_in, gv_in,
     local,
     k_send, k_recv, s_send, s_recv, v_send, v_recv, kf_send, vf_send,
@@ -110,7 +111,7 @@
         def _():
             keys[pl.ds(d * tokens, tokens), :] = jnp.zeros((tokens, width), BF16)
             values[pl.ds(d * tokens, tokens), :] = jnp.zeros((tokens, width), BF16)
-            segs[d] = jnp.zeros((1, tokens), jnp.int32)
+            hots[pl.ds(d * tokens, tokens), :] = jnp.zeros((tokens, width), BF16)
 
     key_load.wait()
     seg_load.wait()
@@ -135,63 +136,117 @@
     def _():
         value_pass_on(0).start()
 
-    for d in range(2, span + 1, 2):
-        @pl.when(me + d < total)
-        def _():
-            value_copy(d).start()
-
-    row_max[...] = jnp.full(row_max.shape, HIDDEN, F32)
+    def one_hot(d):
+        column = jnp.broadcast_to((segs[d] & (width - 1)).astype(F32), (width, tokens)).T
+        lane = lax.broadcasted_iota(jnp.int32, (tokens, width), 1).astype(F32)
+        return jnp.where(column == lane, 1.0, 0.0)
+
     for load in loads_q + loads_g:
         load.wait()
     for h in range(heads):
         stacked = pl.ds(h * tokens, tokens)
+        qt[:, stacked] = qs[stacked, :].T
         gt[:, stacked] = gs[stacked, :].T
+
+    own_hot = one_hot(0)
+    hots[pl.ds(0, tokens), :] = own_hot.astype(BF16)
+    marks_t[...] = (own_hot * SAME).astype(BF16).T
+    row_max[...] = jnp.full(row_max.shape, HIDDEN, F32)
+
+    def score_block(d, diagonal):
+        key_block = jnp.concatenate([keys[rows(d), :], hots[rows(d), :]], axis=1)
+        for h in range(heads):
+            cols = pl.ds(h * tokens, tokens)
+            query = jnp.concatenate([qt[:, cols], marks_t[...]], axis=0)
+            score = dot_nn(key_block, query) * exponent
+            if diagonal:
+                key_at = lax.broadcasted_iota(jnp.int32, (tokens, tokens), 0)
+                query_at = lax.broadcasted_iota(jnp.int32, (tokens, tokens), 1)
+                score = jnp.where(key_at <= query_at, score, HIDDEN)
+            scores[rows(d), cols] = score
+            top = jnp.max(score.reshape(tokens // 8, 8, tokens), axis=0)
+            row_max[:, cols] = jnp.maximum(row_max[:, cols], top)
+
+    score_block(0, True)
 
     def score_pass(s, carry):
         odd = lax.rem(s, 2)
-        d = jnp.where(s == 0, 0, s + 2 * odd - 1)
+        d = s + 2 * odd - 1
         j = lax.div(d, 2) - parity
 
-        @pl.when((d > 0) & (me >= d))
+        @pl.when(me >= d)
         def _():
             key_copy(d).wait_recv()
             seg_copy(d).wait_recv()
+            hots[rows(d), :] = one_hot(d).astype(BF16)
 
         @pl.when((odd == 1) & (me >= d) & (j < half))
         def _():
             key_pass_on(j).start()
 
-        key_block = keys[rows(d), :]
-        seg_column = jnp.broadcast_to(segs[d].astype(F32), (128, tokens)).T
-        seg_key = jnp.concatenate([seg_column] * (tokens // 128), axis=1)
-        key_at = lax.broadcasted_iota(jnp.int32, (tokens, tokens), 0) - d * tokens
-        query_at = lax.broadcasted_iota(jnp.int32, (tokens, tokens), 1)
-        first = jnp.where(me >= d, -d * tokens, tokens)
-        visible = (seg_key == segs[0].astype(F32)) & (key_at <= query_at) & (key_at >= first)
-        bias[...] = jnp.where(visible, 0.0, HIDDEN)
-        for h in range(heads):
-            cols = pl.ds(h * tokens, tokens)
-            score = dot_nt(key_block, qs[cols, :]) + bias[...]
-            top = jnp.max(score, axis=0, keepdims=True)
-            top = jnp.maximum(row_max[0:1, cols], top)
-            part = jnp.exp2((score - top) * exponent)
-            row_max[:, cols] = jnp.broadcast_to(top, (8, tokens))
-            tops[d, :, cols] = jnp.broadcast_to(top, (8, tokens))
-            sums[d, :, cols] = jnp.sum(part.reshape(tokens // 8, 8, tokens), axis=0)
-            probs[rows(d), cols] = part.astype(BF16)
+        for e in range(2, span + 1, 2):
+            @pl.when((s == 1) & (me + e < total))
+            def _():
+                value_copy(e).start()
+
+        score_block(d, False)
         return carry
 
-    lax.fori_loop(0, span + 1, score_pass, 0)
-    for h in range(heads):
+    lax.fori_loop(1, span + 1, score_pass, 0)
+    ones = jnp.ones((16, (span + 1) * tokens), BF16)
+    group = 2 * tokens
+
+    def exp_block(h, d, top):
+        block = pl.ds(d * tokens, tokens)
         cols = pl.ds(h * tokens, tokens)
-        whole = jnp.zeros((8, tokens), F32)
+        probs[block, cols] = jnp.exp2(scores[block, cols] - top).astype(BF16)
+
+    def normalise(h):
+        cols = pl.ds(h * tokens, tokens)
+        inverse = 1.0 / dot_nn(ones, probs[:, cols])[0:1, :]
+        row_inv[:, cols] = jnp.broadcast_to(inverse, (8, tokens))
+        scaled = (gt[:, cols].astype(F32) * inverse).astype(BF16)
+        gt[:, cols] = scaled
+        gs[cols, :] = scaled.T
+
+    def value_grad(i, d):
+        block = pl.ds(d * tokens, tokens)
+        cols = pl.ds(i * group, group)
+        part = dot_nn(probs[block, cols], gs[cols, :])
+        if i > 0:
+            part += value_parts[block, :]
+        value_parts[block, :] = part
+
+    for i in range(heads // 2):
+        e = 2 * i + 2
+        if e <= span:
+            @pl.when(me >= e)
+            def _():
+                value_copy(e).wait_recv()
+
+            @pl.when((me >= e) & (e // 2 - parity < half))
+            def _():
+                value_pass_on(e // 2 - parity).start()
+
+        pair = (2 * i, 2 * i + 1)
+        peaks = [jnp.max(row_max[:, pl.ds(h * tokens, tokens)], axis=0, keepdims=True) for h in pair]
         for d in range(span + 1):
-            part = jnp.exp2((tops[d, :, cols] - row_max[:, cols]) * exponent)
-            tops[d, :, cols] = part
-            whole += part * sums[d, :, cols]
-        inverse = jnp.broadcast_to(1.0 / jnp.sum(whole, axis=0, keepdims=True), (8, tokens))
-        for d in range(span + 1):
-            tops[d, :, cols] *= inverse
+            if i > 0:
+                value_grad(i - 1, d)
+            for h, top in zip(pair, peaks):
+                exp_block(h, d, top)
+        for h in pair:
+            normalise(h)
+    for d in range(span + 1):
+        value_grad(heads // 2 - 1, d)
+    for e in range(heads + 2, span + 1, 2):
+        @pl.when(me >= e)
+        def _():
+            value_copy(e).wait_recv()
+
+        @pl.when((me >= e) & (e // 2 - parity < half))
+        def _():
+            value_pass_on(e // 2 - parity).start()
 
     order = [d for m in range(half, 0, -1) for d in (2 * m - 1, 2 * m)]
     order = [5, 3, 6, 1, 4, 2, 0] if span == 6 else order + [0]
@@ -204,8 +259,8 @@
 
     def hand_out(d, part, odd_ref, pair_ref, out_ref, sum_ref, p_send, p_recv, t_send, into, t_recv):
         sum_ref[...] = part
-        j = lax.div(d, 2)
-        is_odd = lax.rem(d, 2) == 1
+        j = lax.div(jnp.int32(d), 2)
+        is_odd = lax.rem(jnp.int32(d), 2) == 1
 
         @pl.when(is_odd & (me >= d))
         def _():
@@ -224,27 +279,12 @@
             out_ref[j - 1] = sum_ref[...].astype(BF16)
             total_copy(out_ref, into, t_send, t_recv, j - 1).start()
 
-    def value_grad_pass(s, carry):
-        d = block_at(s)
-        e = 2 * s + 2
-
-        @pl.when((s < half) & (me >= e))
-        def _():
-            value_copy(e).wait_recv()
-
-        @pl.when((s < half) & (me >= e) & (s + 1 - parity < half))
-        def _():
-            value_pass_on(s + 1 - parity).start()
-
-        for h in range(heads):
-            cols = pl.ds(h * tokens, tokens)
-            prob = probs[rows(d), cols].astype(F32) * tops[d, 0:1, cols]
-            probs[rows(d), cols] = prob.astype(BF16)
-        part = dot_nn(probs[rows(d), :], gs[...])
-        hand_out(d, part, gv_odd, gv_pair, gv_out, dv_buf, gvp_send, gvp_recv, gv_send, gv_in, gv_recv)
-        return carry
-
-    lax.fori_loop(0, span + 1, value_grad_pass, 0)
+    def value_hand_out(d):
+        hand_out(d, value_parts[rows(d), :], gv_odd, gv_pair, gv_out, dv_buf,
+                 gvp_send, gvp_recv, gv_send, gv_in, gv_recv)
+
+    for d in range(span - 1, 0, -2):
+        value_hand_out(d)
     for d in range(1, span + 1, 2):
         @pl.when(me >= d)
         def _():
@@ -254,20 +294,23 @@
     for h in range(heads):
         cols = pl.ds(h * tokens, tokens)
         head = pl.ds(h * width, width)
-        attended = dot_nn(values_t, probs[:, cols]).astype(BF16)
+        attended = (dot_nn(values_t, probs[:, cols]) * row_inv[0:1, cols]).astype(BF16)
         dot = jnp.sum(attended.astype(F32) * gt[:, cols].astype(F32), axis=0, keepdims=True)
         row_dot[:, cols] = jnp.broadcast_to(dot, (8, tokens))
         o_buf[:, head] = attended.T
+
+    for d in range(span, -1, -2):
+        value_hand_out(d)
 
     def key_grad_pass(s, carry):
         d = block_at(s)
         value_block = values[rows(d), :]
         for h in range(heads):
             cols = pl.ds(h * tokens, tokens)
-            dprob = dot_nt(value_block, gs[cols, :])
+            dprob = dot_nn(value_block, gt[:, cols])
             prob = probs[rows(d), cols].astype(F32)
-            probs[rows(d), cols] = (prob * (dprob - row_dot[0:1, cols])).astype(BF16)
-        part = dot_nn(probs[rows(d), :], qs[...]) * scale
+            dscores[rows(d), cols] = (prob * (dprob - row_dot[0:1, cols])).astype(BF16)
+        part = dot_nn(dscores[rows(d), :], qs[...]) * scale
         hand_out(d, part, gk_odd, gk_pair, gk_out, dk_buf, gkp_send, gkp_recv, gk_send, gk_in, gk_recv)
         return carry
 
@@ -275,7 +318,7 @@
     keys_t = keys[...].T
     for h in range(heads):
         cols = pl.ds(h * tokens, tokens)
-        grad = (dot_nn(keys_t, probs[:, cols]) * scale).astype(BF16)
+        grad = (dot_nn(keys_t, dscores[:, cols]) * scale).astype(BF16)
         dq_buf[:, pl.ds(h * width, width)] = grad.T
 
     for j in range(half - 1, -1, -1):
@@ -346,11 +389,15 @@
             pltpu.VMEM((stacked, width), BF16),
             pltpu.VMEM((stacked, width), BF16),
             pltpu.VMEM((width, stacked), BF16),
-            pltpu.VMEM((tokens, tokens), F32),
+            pltpu.VMEM((width, stacked), BF16),
+            pltpu.VMEM((blocks * tokens, width), BF16),
+            pltpu.VMEM((width, tokens), BF16),
+            pltpu.VMEM((blocks * tokens, stacked), F32),
             pltpu.VMEM((blocks * tokens, stacked), BF16),
+            pltpu.VMEM((blocks * tokens, stacked), BF16),
+            pltpu.VMEM((blocks * tokens, width), F32),
             pltpu.VMEM((8, stacked), F32),
-            pltpu.VMEM((blocks, 8, stacked), F32),
-            pltpu.VMEM((blocks, 8, stacked), F32),
+            pltpu.VMEM((8, stacked), F32),
             pltpu.VMEM((8, stacked), F32),
         ]
         + [block] * 8
@@ -358,7 +405,7 @@
         + [sem((blocks,))] * 6
         + [sem((half,))] * 10,
         compiler_params=pltpu.CompilerParams(
-            collective_id=0, has_side_effects=True, vmem_limit_bytes=40 * 1024 * 1024
+            collective_id=0, has_side_effects=True, vmem_limit_bytes=48 * 1024 * 1024
         ),
     )(*[
         pltpu.with_memory_space_constraint(a, pltpu.HBM)

time: 31.6 us -> 32.8 us (1.038)
  the two profiles are of different devices: /device:TPU:7 before, /device:TPU:22 now
where the time goes in v3:
time: 32.8 us; the launch traced here: 32.7 us
  Pallas kernels  32 us (98%)
  between operations  0.64 us (2%)
    pallas_call x1, Pallas kernels, on_device(): pl.pallas_call(functools.partial(kernel, groups, total, span), out_shape=...  30.9 us
    pallas_call x1, Pallas kernels, write_back(): pl.pallas_call(store, out_shape=tuple((jax.ShapeDtypeStruct(r.shape, r.dt...  1.08 us

profile of v3, /device:TPU:22, one launch (start us, length us, event | category | flops | bytes accessed | tf_op | source)
XLA Modules:
  0.0 32.7 jit_solution(13272051768988100995)
XLA Ops:
  0.6 30.9 %shard_map.84 = (bf16[256,1024]{1,0:T(8,128)(2,1)S(1)}, bf16[256,1024]{1,0:T(8,128)(2,1)S(1)}, f32[256,128]{1,0:T(8,128)S(1)}, f32[256,128]{1,0:T(8,128)S(1)}) custom-call(bf16[256,1024]{1,0:T(8,128)(2,1)} %q_hbm.1, bf16[256,128]{1,0:T(8,128)(2,1)} %k_hbm.1, bf16[256,128]{1,0:T(8,128)(2,1)} %v_hbm.1, bf16[256,1024]{1,0:T(8,128)(2,1)} %g_hbm.1, s32[1,256]{1,0:T(1,128)} %bitcast.1), custom_call_target="tpu_custom_call" | custom-call | tf_op jit(solution)/shard_map/pallas_call | solution.py:375
  31.6 1.1 %shard_map.85 = (bf16[256,1024]{1,0:T(8,128)(2,1)}, bf16[256,1024]{1,0:T(8,128)(2,1)}, f32[256,128]{1,0:T(8,128)}, f32[256,128]{1,0:T(8,128)}) custom-call(bf16[256,1024]{1,0:T(8,128)(2,1)S(1)} %get-tuple-element.8.refs_0_, bf16[256,1024]{1,0:T(8,128)(2,1)S(1)} %get-tuple-element.9.refs_1_, f32[256,128]{1,0:T(8,128)S(1)} %get-tuple-element.10.refs_2_, ...), custom_call_target="tpu_custom_call" | custom-call | tf_op jit(solution)/shard_map/pallas_call | solution.py:429

commit v4 on v3

--- a/solution.py
+++ b/solution.py
@@ -118,6 +118,11 @@
     value_load.wait()
     pl.semaphore_wait(barrier, expected)
 
+    for d in range(1, span + 1):
+        @pl.when(me + d < total)
+        def _():
+            seg_copy(d).start()
+
     @pl.when(parity == 0)
     def _():
         key_pass_on(0).start()
@@ -126,11 +131,6 @@
         @pl.when(me + d < total)
         def _():
             key_copy(d).start()
-
-    for d in range(1, span + 1):
-        @pl.when(me + d < total)
-        def _():
-            seg_copy(d).start()
 
     @pl.when(parity == 0)
     def _():
@@ -140,6 +140,11 @@
         column = jnp.broadcast_to((segs[d] & (width - 1)).astype(F32), (width, tokens)).T
         lane = lax.broadcasted_iota(jnp.int32, (tokens, width), 1).astype(F32)
         return jnp.where(column == lane, 1.0, 0.0)
+
+    for e in range(2, span + 1, 2):
+        @pl.when(me + e < total)
+        def _():
+            value_copy(e).start()
 
     for load in loads_q + loads_g:
         load.wait()
@@ -170,9 +175,9 @@
     score_block(0, True)
 
     def score_pass(s, carry):
-        odd = lax.rem(s, 2)
-        d = s + 2 * odd - 1
-        j = lax.div(d, 2) - parity
+        direct = s <= half
+        d = jnp.where(direct, 2 * s, 2 * (s - half) - 1)
+        j = s - parity
 
         @pl.when(me >= d)
         def _():
@@ -180,14 +185,9 @@
             seg_copy(d).wait_recv()
             hots[rows(d), :] = one_hot(d).astype(BF16)
 
-        @pl.when((odd == 1) & (me >= d) & (j < half))
+        @pl.when(direct & (me >= d) & (j < half))
         def _():
             key_pass_on(j).start()
-
-        for e in range(2, span + 1, 2):
-            @pl.when((s == 1) & (me + e < total))
-            def _():
-                value_copy(e).start()
 
         score_block(d, False)
         return carry
@@ -298,9 +298,9 @@
         dot = jnp.sum(attended.astype(F32) * gt[:, cols].astype(F32), axis=0, keepdims=True)
         row_dot[:, cols] = jnp.broadcast_to(dot, (8, tokens))
         o_buf[:, head] = attended.T
-
-    for d in range(span, -1, -2):
-        value_hand_out(d)
+        if h == heads // 2 - 1:
+            for d in range(span, -1, -2):
+                value_hand_out(d)
 
     def key_grad_pass(s, carry):
         d = block_at(s)

time: 32.8 us -> 30.9 us (0.942)
  the two profiles are of different devices: /device:TPU:22 before, /device:TPU:7 now
where the time goes in v4:
time: 30.9 us; the launch traced here: 30.7 us
  Pallas kernels  30 us (97%)
  between operations  0.64 us (2%)
    pallas_call x1, Pallas kernels, on_device(): pl.pallas_call(functools.partial(kernel, groups, total, span), out_shape=...  28.9 us
    pallas_call x1, Pallas kernels, write_back(): pl.pallas_call(store, out_shape=tuple((jax.ShapeDtypeStruct(r.shape, r.dt...  1.08 us

profile of v4, /device:TPU:7, one launch (start us, length us, event | category | flops | bytes accessed | tf_op | source)
XLA Modules:
  0.0 30.7 jit_solution(5625128413110973550)
XLA Ops:
  0.6 28.9 %shard_map.84 = (bf16[256,1024]{1,0:T(8,128)(2,1)S(1)}, bf16[256,1024]{1,0:T(8,128)(2,1)S(1)}, f32[256,128]{1,0:T(8,128)S(1)}, f32[256,128]{1,0:T(8,128)S(1)}) custom-call(bf16[256,1024]{1,0:T(8,128)(2,1)} %q_hbm.1, bf16[256,128]{1,0:T(8,128)(2,1)} %k_hbm.1, bf16[256,128]{1,0:T(8,128)(2,1)} %v_hbm.1, bf16[256,1024]{1,0:T(8,128)(2,1)} %g_hbm.1, s32[1,256]{1,0:T(1,128)} %bitcast.1), custom_call_target="tpu_custom_call" | custom-call | tf_op jit(solution)/shard_map/pallas_call | solution.py:375
  29.6 1.1 %shard_map.85 = (bf16[256,1024]{1,0:T(8,128)(2,1)}, bf16[256,1024]{1,0:T(8,128)(2,1)}, f32[256,128]{1,0:T(8,128)}, f32[256,128]{1,0:T(8,128)}) custom-call(bf16[256,1024]{1,0:T(8,128)(2,1)S(1)} %get-tuple-element.8.refs_0_, bf16[256,1024]{1,0:T(8,128)(2,1)S(1)} %get-tuple-element.9.refs_1_, f32[256,128]{1,0:T(8,128)S(1)} %get-tuple-element.10.refs_2_, ...), custom_call_target="tpu_custom_call" | custom-call | tf_op jit(solution)/shard_map/pallas_call | solution.py:429

commit v5 on v4

--- a/solution.py
+++ b/solution.py
@@ -31,8 +31,8 @@
     o_buf, dq_buf, dk_buf, dv_buf,
     keys, values, segs, qs, gs, qt, gt, hots, marks_t, scores, probs, dscores, value_parts,
     row_max, row_inv, row_dot,
-    gk_odd, gv_odd, gk_pair, gv_pair, gk_out, gv_out, gk_in, gv_in,
-    local,
+    gk_odd, gv_odd, gk_pair, gv_pair, gk_out, gv_out, gk_in, gv_in, gv_hop,
+    local, hop_send, hop_recv,
     k_send, k_recv, s_send, s_recv, v_send, v_recv, kf_send, vf_send,
     gkp_send, gkp_recv, gvp_send, gvp_recv, gk_send, gk_recv, gv_send, gv_recv,
 ):
@@ -45,6 +45,13 @@
     parity = lax.rem(me, 2)
     partner = me + 1 - 2 * parity
 
+    plane = 2 * groups
+    hops = plane == 8 and total % plane == 0 and span == 6
+    seat = lax.rem(me, plane)
+    gives = (seat < 2) if hops else (seat < 0)
+    takes = (seat >= 4) & (me >= plane)
+    seat_slot = jnp.where(seat >= 6, 0, 1)
+
     def at(where):
         return (lax.div(where, groups), lax.rem(where, groups))
 
@@ -79,9 +86,15 @@
     def total_copy(out, into, send, recv, j):
         return remote(out.at[j], into.at[j], send.at[j], recv.at[j], me - 2 * (j + 1))
 
+    def give_copy(j):
+        return remote(gv_out.at[j], gv_hop, gv_send.at[j], hop_recv, me + plane - 2 * (j + 1))
+
+    def take_copy():
+        return remote(gv_hop, gv_in.at[seat_slot], hop_send, gv_recv.at[seat_slot], me - plane)
+
     barrier = pltpu.get_barrier_semaphore()
     expected = 0
-    for d in range(1, span + 1):
+    for d in [*range(1, span + 1)] + ([plane] if hops else []):
         for way in (d, -d):
             inside = (me + way >= 0) & (me + way < total)
             expected = expected + inside.astype(jnp.int32)
@@ -257,7 +270,7 @@
             d = jnp.where(s == i, order[i], d)
         return d
 
-    def hand_out(d, part, odd_ref, pair_ref, out_ref, sum_ref, p_send, p_recv, t_send, into, t_recv):
+    def hand_out(d, part, odd_ref, pair_ref, out_ref, sum_ref, p_send, p_recv, t_send, into, t_recv, hop):
         sum_ref[...] = part
         j = lax.div(jnp.int32(d), 2)
         is_odd = lax.rem(jnp.int32(d), 2) == 1
@@ -277,11 +290,18 @@
         @pl.when(jnp.logical_not(is_odd) & (d > 0) & (me >= d))
         def _():
             out_ref[j - 1] = sum_ref[...].astype(BF16)
-            total_copy(out_ref, into, t_send, t_recv, j - 1).start()
+
+            @pl.when(gives & hop & (d < span))
+            def _():
+                give_copy(j - 1).start()
+
+            @pl.when(jnp.logical_not(gives & hop & (d < span)))
+            def _():
+                total_copy(out_ref, into, t_send, t_recv, j - 1).start()
 
     def value_hand_out(d):
         hand_out(d, value_parts[rows(d), :], gv_odd, gv_pair, gv_out, dv_buf,
-                 gvp_send, gvp_recv, gv_send, gv_in, gv_recv)
+                 gvp_send, gvp_recv, gv_send, gv_in, gv_recv, hops)
 
     for d in range(span - 1, 0, -2):
         value_hand_out(d)
@@ -304,6 +324,12 @@
 
     def key_grad_pass(s, carry):
         d = block_at(s)
+        if hops:
+            @pl.when((s == span) & takes)
+            def _():
+                give_copy(0).wait_recv()
+                take_copy().start()
+
         value_block = values[rows(d), :]
         for h in range(heads):
             cols = pl.ds(h * tokens, tokens)
@@ -311,7 +337,7 @@
             prob = probs[rows(d), cols].astype(F32)
             dscores[rows(d), cols] = (prob * (dprob - row_dot[0:1, cols])).astype(BF16)
         part = dot_nn(dscores[rows(d), :], qs[...]) * scale
-        hand_out(d, part, gk_odd, gk_pair, gk_out, dk_buf, gkp_send, gkp_recv, gk_send, gk_in, gk_recv)
+        hand_out(d, part, gk_odd, gk_pair, gk_out, dk_buf, gkp_send, gkp_recv, gk_send, gk_in, gk_recv, False)
         return carry
 
     lax.fori_loop(0, span + 1, key_grad_pass, 0)
@@ -334,6 +360,10 @@
             dk_buf[...] += gk_in[j].astype(F32)
 
 
+    if hops:
+        @pl.when(takes)
+        def _():
+            take_copy().wait_send()
     for d in range(1, span + 1):
         @pl.when(me + d < total)
         def _():
@@ -401,7 +431,8 @@
             pltpu.VMEM((8, stacked), F32),
         ]
         + [block] * 8
-        + [sem((3 + 2 * heads,))]
+        + [pltpu.VMEM((tokens, width), BF16)]
+        + [sem((3 + 2 * heads,)), sem, sem]
         + [sem((blocks,))] * 6
         + [sem((half,))] * 10,
         compiler_params=pltpu.CompilerParams(

time: 30.9 us -> 30.3 us (0.981)
  Pallas kernels: 30 us -> 29.5 us
    pallas_call x1, Pallas kernels: 28.9 us -> 28.4 us  [on_device(): pl.pallas_call(functools.partial(kernel, groups, total, span), out_shape=...]
where the time goes in v5:
time: 30.3 us; the launch traced here: 30.1 us
  Pallas kernels  29.5 us (97%)
  between operations  0.64 us (2%)
    pallas_call x1, Pallas kernels, on_device(): pl.pallas_call(functools.partial(kernel, groups, total, span), out_shape=...  28.4 us
    pallas_call x1, Pallas kernels, write_back(): pl.pallas_call(store, out_shape=tuple((jax.ShapeDtypeStruct(r.shape, r.dt...  1.08 us

profile of v5, /device:TPU:7, one launch (start us, length us, event | category | flops | bytes accessed | tf_op | source)
XLA Modules:
  0.0 30.1 jit_solution(7090878391868330046)
XLA Ops:
  0.6 28.4 %shard_map.84 = (bf16[256,1024]{1,0:T(8,128)(2,1)S(1)}, bf16[256,1024]{1,0:T(8,128)(2,1)S(1)}, f32[256,128]{1,0:T(8,128)S(1)}, f32[256,128]{1,0:T(8,128)S(1)}) custom-call(bf16[256,1024]{1,0:T(8,128)(2,1)} %q_hbm.1, bf16[256,128]{1,0:T(8,128)(2,1)} %k_hbm.1, bf16[256,128]{1,0:T(8,128)(2,1)} %v_hbm.1, bf16[256,1024]{1,0:T(8,128)(2,1)} %g_hbm.1, s32[1,256]{1,0:T(1,128)} %bitcast.1), custom_call_target="tpu_custom_call" | custom-call | tf_op jit(solution)/shard_map/pallas_call | solution.py:405
  29.0 1.1 %shard_map.85 = (bf16[256,1024]{1,0:T(8,128)(2,1)}, bf16[256,1024]{1,0:T(8,128)(2,1)}, f32[256,128]{1,0:T(8,128)}, f32[256,128]{1,0:T(8,128)}) custom-call(bf16[256,1024]{1,0:T(8,128)(2,1)S(1)} %get-tuple-element.8.refs_0_, bf16[256,1024]{1,0:T(8,128)(2,1)S(1)} %get-tuple-element.9.refs_1_, f32[256,128]{1,0:T(8,128)S(1)} %get-tuple-element.10.refs_2_, ...), custom_call_target="tpu_custom_call" | custom-call | tf_op jit(solution)/shard_map/pallas_call | solution.py:460

commit v6 on v5

--- a/solution.py
+++ b/solution.py
@@ -262,7 +262,7 @@
             value_pass_on(e // 2 - parity).start()
 
     order = [d for m in range(half, 0, -1) for d in (2 * m - 1, 2 * m)]
-    order = [5, 3, 6, 1, 4, 2, 0] if span == 6 else order + [0]
+    order = [5, 6, 3, 4, 1, 2, 0] if span == 6 else order + [0]
 
     def block_at(s):
         d = order[-1]

time: 30.3 us -> 30 us (0.990); the launches traced: 30.1 us -> 29.4 us
  Pallas kernels: 29.5 us -> 28.7 us
    pallas_call x1, Pallas kernels: 28.4 us -> 27.6 us  [on_device(): pl.pallas_call(functools.partial(kernel, groups, total, span), out_shape=...]
where the time goes in v6:
time: 30 us; the launch traced here: 29.4 us
  Pallas kernels  28.7 us (96%)
  between operations  0.64 us (2%)
    pallas_call x1, Pallas kernels, on_device(): pl.pallas_call(functools.partial(kernel, groups, total, span), out_shape=...  27.6 us
    pallas_call x1, Pallas kernels, write_back(): pl.pallas_call(store, out_shape=tuple((jax.ShapeDtypeStruct(r.shape, r.dt...  1.08 us

profile of v6, /device:TPU:7, one launch (start us, length us, event | category | flops | bytes accessed | tf_op | source)
XLA Modules:
  0.0 29.4 jit_solution(3807359542604064214)
XLA Ops:
  0.6 27.6 %shard_map.84 = (bf16[256,1024]{1,0:T(8,128)(2,1)S(1)}, bf16[256,1024]{1,0:T(8,128)(2,1)S(1)}, f32[256,128]{1,0:T(8,128)S(1)}, f32[256,128]{1,0:T(8,128)S(1)}) custom-call(bf16[256,1024]{1,0:T(8,128)(2,1)} %q_hbm.1, bf16[256,128]{1,0:T(8,128)(2,1)} %k_hbm.1, bf16[256,128]{1,0:T(8,128)(2,1)} %v_hbm.1, bf16[256,1024]{1,0:T(8,128)(2,1)} %g_hbm.1, s32[1,256]{1,0:T(1,128)} %bitcast.1), custom_call_target="tpu_custom_call" | custom-call | tf_op jit(solution)/shard_map/pallas_call | solution.py:405
  28.3 1.1 %shard_map.85 = (bf16[256,1024]{1,0:T(8,128)(2,1)}, bf16[256,1024]{1,0:T(8,128)(2,1)}, f32[256,128]{1,0:T(8,128)}, f32[256,128]{1,0:T(8,128)}) custom-call(bf16[256,1024]{1,0:T(8,128)(2,1)S(1)} %get-tuple-element.8.refs_0_, bf16[256,1024]{1,0:T(8,128)(2,1)S(1)} %get-tuple-element.9.refs_1_, f32[256,128]{1,0:T(8,128)S(1)} %get-tuple-element.10.refs_2_, ...), custom_call_target="tpu_custom_call" | custom-call | tf_op jit(solution)/shard_map/pallas_call | solution.py:460

commit v7 on v6

--- a/solution.py
+++ b/solution.py
@@ -318,7 +318,7 @@
         dot = jnp.sum(attended.astype(F32) * gt[:, cols].astype(F32), axis=0, keepdims=True)
         row_dot[:, cols] = jnp.broadcast_to(dot, (8, tokens))
         o_buf[:, head] = attended.T
-        if h == heads // 2 - 1:
+        if h == heads - 1:
             for d in range(span, -1, -2):
                 value_hand_out(d)
 

time: 30 us -> 29.7 us (0.990)
  the two profiles are of different devices: /device:TPU:7 before, /device:TPU:5 now
where the time goes in v7:
time: 29.7 us; the launch traced here: 29.5 us
  Pallas kernels  28.9 us (97%)
  between operations  0.64 us (2%)
    pallas_call x1, Pallas kernels, on_device(): pl.pallas_call(functools.partial(kernel, groups, total, span), out_shape=...  27.8 us
    pallas_call x1, Pallas kernels, write_back(): pl.pallas_call(store, out_shape=tuple((jax.ShapeDtypeStruct(r.shape, r.dt...  1.08 us

profile of v7, /device:TPU:5, one launch (start us, length us, event | category | flops | bytes accessed | tf_op | source)
XLA Modules:
  0.0 29.5 jit_solution(9496453104849924377)
XLA Ops:
  0.6 27.8 %shard_map.84 = (bf16[256,1024]{1,0:T(8,128)(2,1)S(1)}, bf16[256,1024]{1,0:T(8,128)(2,1)S(1)}, f32[256,128]{1,0:T(8,128)S(1)}, f32[256,128]{1,0:T(8,128)S(1)}) custom-call(bf16[256,1024]{1,0:T(8,128)(2,1)} %q_hbm.1, bf16[256,128]{1,0:T(8,128)(2,1)} %k_hbm.1, bf16[256,128]{1,0:T(8,128)(2,1)} %v_hbm.1, bf16[256,1024]{1,0:T(8,128)(2,1)} %g_hbm.1, s32[1,256]{1,0:T(1,128)} %bitcast.1), custom_call_target="tpu_custom_call" | custom-call | tf_op jit(solution)/shard_map/pallas_call | solution.py:405
  28.4 1.1 %shard_map.85 = (bf16[256,1024]{1,0:T(8,128)(2,1)}, bf16[256,1024]{1,0:T(8,128)(2,1)}, f32[256,128]{1,0:T(8,128)}, f32[256,128]{1,0:T(8,128)}) custom-call(bf16[256,1024]{1,0:T(8,128)(2,1)S(1)} %get-tuple-element.8.refs_0_, bf16[256,1024]{1,0:T(8,128)(2,1)S(1)} %get-tuple-element.9.refs_1_, f32[256,128]{1,0:T(8,128)S(1)} %get-tuple-element.10.refs_2_, ...), custom_call_target="tpu_custom_call" | custom-call | tf_op jit(solution)/shard_map/pallas_call | solution.py:460
